TPU v7x, 256 devices: a whole 4x4x8 slice. The times are simulated.
256 devices in a mesh: paths: 8 (over x, core), cpty: 32 (over z, y).
Axes of the slice: x: 4, y: 4, z: 8, core: 2. Of those that a mesh axis runs over, the one named last changes fastest.
Arguments:
- factors: bfloat16 [64, 12288], P(None, 'paths'), may hold values from -6 to 6
- loadings: bfloat16 [64, 65536], P(None, 'cpty'), may hold values from -2 to 2
- notional: bfloat16 [65536], P('cpty'), may hold values from 0.25 to 0.796875
- strike: bfloat16 [65536], P('cpty'), may hold values from 2 to 8
- curvature: bfloat16 [65536], P('cpty'), may hold values from 1 to 3
- trade_cpty: int32 [65536], P('cpty'), may hold values from 0 to 4095, as said below
Outputs:
- exposure: bfloat16 [12288, 4096], P('paths', 'cpty')
- moment: float32 [4096, 4096], P('paths', 'cpty')
Inputs may be any that keep to these rules, and one draw needn't show every extreme that they name: `trade_cpty`: of the trades in the book of one index of cpty, at most 128 belong to the counterparties numbered k * 128 to (k + 1) * 128 - 1 for any k; in every draw some such k receives exactly 128 from every book.
All inputs are finite; a program needn't handle non-finite values.
Results may differ from a plain program's by a relative error of at most 0.0064.
Values may be sent and summed in bfloat16 or wider, within the bound.
A program may use at most 128 MiB of HBM per device.

v0:
```python
import jax
import jax.numpy as jnp
from jax import lax
from jax.sharding import PartitionSpec as P

CP_DEV = 128


def in_blocks(x, dim, length):
    before, after = (x.shape[:dim], x.shape[dim + 1 :])
    return jnp.moveaxis(x.reshape(*before, length, -1, *after), dim, 0)


def summed_on_arrival(x, axis, dim):
    parts = in_blocks(x, dim, lax.axis_size(axis))
    arrived = lax.all_to_all(parts, axis, split_axis=0, concat_axis=0, tiled=True)
    return arrived.astype(jnp.float32).sum(axis=0)


def price_trades(drivers, loading_cols, trade_terms):
    linear = jnp.dot(drivers, loading_cols, preferred_element_type=jnp.float32)
    terms_wide = trade_terms.astype(jnp.float32)
    value = terms_wide[0] * (linear + terms_wide[2] * jnp.tanh(linear - terms_wide[1]))
    return value.astype(jnp.bfloat16)


def on_device(factors, loadings, notional, strike, curvature, trade_cpty):
    groups = lax.axis_size("cpty")
    own_index = lax.axis_index("cpty")
    trades = loadings.shape[1]
    slot_size = 2 * trades // groups
    owners = trade_cpty // CP_DEV
    marked = (owners[:, None] == jnp.arange(groups, dtype=jnp.int32)[None, :]).astype(jnp.int32)
    ranking = jnp.sum((jnp.cumsum(marked, axis=0) - marked) * marked, axis=1)
    target = owners * slot_size + ranking
    chosen = (
        jnp.zeros((groups * slot_size,), jnp.int32)
        .at[target]
        .set(jnp.arange(trades, dtype=jnp.int32))
    )
    filled = jnp.zeros((groups * slot_size,), jnp.bool_).at[target].set(True)
    labels = jnp.where(filled, trade_cpty[chosen], -1)[None, :]
    drivers = jnp.transpose(factors)
    trade_terms = jnp.stack([notional, strike, curvature])
    described = jnp.concatenate([loadings, trade_terms], axis=0)
    packed = jnp.where(
        filled[None, :], jnp.take(described, chosen, axis=1), jnp.zeros((), jnp.bfloat16)
    )
    received, arrived_ids = (
        lax.all_to_all(packed, "cpty", split_axis=1, concat_axis=1, tiled=True),
        lax.all_to_all(labels, "cpty", split_axis=1, concat_axis=1, tiled=True),
    )
    factor_count = loadings.shape[0]
    arrived = price_trades(drivers, received[:factor_count], received[factor_count:])
    local_ids = arrived_ids[0] - own_index * CP_DEV
    onehot = (local_ids[:, None] == jnp.arange(CP_DEV, dtype=jnp.int32)[None, :]).astype(
        jnp.bfloat16
    )
    netted = jnp.dot(arrived, onehot, preferred_element_type=jnp.float32)
    exposure = jnp.maximum(netted, 0.0).astype(jnp.bfloat16)
    everyone = lax.all_gather(exposure, "cpty", axis=1, tiled=True)
    path_total = exposure.shape[0] * lax.axis_size("paths")
    moment = (
        summed_on_arrival(
            jnp.einsum("pa,pb->ab", everyone, exposure, preferred_element_type=jnp.float32).astype(
                jnp.bfloat16
            ),
            "paths",
            0,
        )
        / path_total
    )
    return (exposure, moment)


def solution(mesh):
    in_specs = (P(None, "paths"), P(None, "cpty"), P("cpty"), P("cpty"), P("cpty"), P("cpty"))
    out_specs = (P("paths", "cpty"), P("paths", "cpty"))
    return jax.shard_map(
        on_device, mesh=mesh, in_specs=in_specs, out_specs=out_specs, check_vma=False
    )
```

profile of v0, /device:TPU:1, one launch (start us, length us, event | category | flops | bytes accessed | tf_op | source)
XLA Modules:
  0.0 287.2 jit_solution(17059434159926769436)
XLA Ops:
  7.2 0.8 add_select_fusion
  8.0 9.1 %reduce-window.6 = s32[32,16,128]{2,1,0:T(8,128)S(1)} reduce-window(s32[32,16,128]{2,1,0:T(8,128)S(1)} %fusion.18, s32[]{:T(128)} %constant.24.clone.1), window={size=1x1x128 pad=0_0x0_0x127_0}, to_apply=%region_0.1 | reduce-window | flops 8323072 | bytes 524292 | tf_op jit(solution)/shard_map/reduce-window
  17.1 0.1 slice.40
  17.2 0.2 copy.33
  17.5 0.2 reduce-window.9
  17.7 0.1 broadcast_add_fusion
  17.8 0.1 fusion.17
  17.9 0.7 compare_select_fusion.1
  18.7 8.1 %scatter_custom_fusion.1 = s32[4096]{0:T(1024)S(1)} fusion(s32[2048]{0:T(1024)S(1)} %compare_select_fusion.1, s32[2048]{0:T(1024)S(1)} %iota.15, s32[]{:T(128)} %constant.24.clone.1), kind=kCustom, calls=%fused_computation.49 | custom fusion | bytes 16388 | tf_op jit(solution)/shard_map/scatter | solution.py:39
  26.7 23.0 %gather_fusion.1 = s32[4096]{0:T(1024)S(1)} fusion(s32[2048]{0:T(1024)S(1)} %copy-done.1, s32[4096]{0:T(1024)S(1)} %fusion.19), kind=kCustom, calls=%fused_computation.1 | custom fusion | bytes 49152 | tf_op jit(solution)/shard_map/gather | solution.py:42
  49.8 9.1 %scatter_custom_fusion = pred[4096]{0:T(1024)(128)(4,1)S(1)} fusion(s32[2048]{0:T(1024)S(1)} %compare_select_fusion.1, pred[2048]{0:T(1024)(128)(4,1)S(1)} %broadcast.49, pred[]{:T(512)} %constant.22.clone.1), kind=kCustom, calls=%fused_computation.53 | custom fusion | bytes 4097 | tf_op jit(solution)/shard_map/scatter | solution.py:41
  58.9 0.6 broadcast_select_fusion
  59.5 12.0 %all-to-all-start.1 = ((s32[1,32,128]{2,0,1:T(1,128)}), s32[1,32,128]{2,0,1:T(1,128)S(1)}, u32[]{:S(2)}, u32[]{:S(2)}) async-start(s32[1,32,128]{2,0,1:T(1,128)} %bitcast.12), calls=%async_computation.1 | async-start | bytes 32768 | tf_op jit(solution)/shard_map/all_to_all | solution.py:51
  71.6 0.3 copy.26
  71.9 0.3 stack.12
  72.3 0.3 stack.13
  72.6 0.3 stack.14
  72.9 0.7 pad_maximum_fusion
  73.7 12.1 %gather_fusion = bf16[4096,67]{1,0:T(8,128)(2,1)S(1)} fusion(bf16[67,2048]{0,1:T(8,128)(2,1)S(1)} %pad_maximum_fusion, s32[4096]{0:T(1024)S(1)} %fusion.19), kind=kCustom, calls=%fused_computation | custom fusion | bytes 1114112 | tf_op jit(solution)/shard_map/jit(_take)/gather | solution.py:47
  85.8 0.6 copy.30
  86.4 0.9 select_select_fusion
  87.3 9.2 %all-to-all-start = ((bf16[67,32,128]{2,0,1:T(8,128)(2,1)}), bf16[67,32,128]{2,0,1:T(8,128)(2,1)S(1)}, u32[]{:S(2)}, u32[]{:S(2)}) async-start(bf16[67,32,128]{2,0,1:T(8,128)(2,1)} %select_select_fusion), calls=%async_computation | async-start | bytes 1179648 | tf_op jit(solution)/shard_map/all_to_all | solution.py:50
  96.6 0.0 all-gather.2.cloned.1.call-start
  96.6 0.9 iota_compare_fusion.7
  97.5 15.6 %all-to-all-done = bf16[67,32,128]{2,0,1:T(8,128)(2,1)S(1)} async-done(((bf16[67,32,128]{2,0,1:T(8,128)(2,1)}), bf16[67,32,128]{2,0,1:T(8,128)(2,1)S(1)}, u32[]{:S(2)}, u32[]{:S(2)}) %all-to-all-start) | async-done | bytes 548896 | tf_op jit(solution)/shard_map/all_to_all | solution.py:50
  113.2 14.0 %fusion.9 = bf16[1536,128]{1,0:T(8,128)(2,1)} fusion(bf16[64,1536]{1,0:T(8,128)(2,1)S(1)} %copy-done, f32[4096]{0:T(1024)S(1)} %get-tuple-element.3, f32[4096]{0:T(1024)S(1)} %get-tuple-element.4, f32[4096]{0:T(1024)S(1)} %get-tuple-element.2, bf16[67,32,128]{2,0,1:T(8,128)(2,1)S(1)} %all-to-all-done, pred[4096,128]{1,0:T(32,128)(4,1)S(1)} %iota_compare_fusion.7), kind=kOutput, calls=%fused_computation.16 | convolution fusion | flops 2447769600 | bytes 1687552 | tf_op jit(solution)/shard_map/dot_general | solution.py:59
  127.2 0.0 all-gather.2.cloned.1.call-update
  127.2 121.3 %all-gather.2.cloned.1.call-done = bf16[1536,4096]{1,0:T(8,128)(2,1)} async-done(((bf16[1536,128]{1,0:T(8,128)(2,1)}), bf16[1536,4096]{1,0:T(8,128)(2,1)}) %all-gather.2.cloned.1.call-update) | async-done | bytes 12582928 | tf_op jit(solution)/shard_map/all_gather | solution.py:61
  248.5 8.1 %convolution_convert_fusion = bf16[4096,128]{1,0:T(8,128)(2,1)S(1)} fusion(bf16[1536,4096]{1,0:T(8,128)(2,1)} %all-gather.2.cloned.1.call-done, bf16[1536,128]{1,0:T(8,128)(2,1)} %fusion.9), kind=kOutput, calls=%fused_computation.14 | convolution fusion | flops 1611137024 | bytes 14024704 | tf_op jit(solution)/shard_map/pa,pb->ab/dot_general | solution.py:65
  256.5 23.0 %all_to_all.20 = bf16[8,512,128]{2,1,0:T(8,128)(2,1)S(1)} all-to-all(bf16[8,512,128]{2,1,0:T(8,128)(2,1)S(1)} %bitcast.86), channel_id=1, replica_groups=mesh['paths'=8,'cpty'=32] {'paths'}, dimensions={0} | all-to-all | bytes 2097152 | tf_op jit(solution)/shard_map/all_to_all | solution.py:16
  279.5 0.1 convert_reduce_fusion
  279.6 0.7 broadcast_multiply_fusion
  (22 shorter events, 0.1 us)
Async XLA Ops:
  7.2 106.0 %copy-start = (bf16[64,1536]{1,0:T(8,128)(2,1)S(1)}, bf16[64,1536]{1,0:T(8,128)(2,1)}, u32[]{:S(2)}) copy-start(bf16[64,1536]{1,0:T(8,128)(2,1)} %param.6) | copy-start | bytes 589828
  7.2 19.6 %copy-start.1 = (s32[2048]{0:T(1024)S(1)}, s32[2048]{0:T(1024)}, u32[]{:S(2)}) copy-start(s32[2048]{0:T(1024)} %param.11) | copy-start | bytes 24580
  7.2 64.4 %copy-start.2 = (bf16[64,2048]{1,0:T(8,128)(2,1)S(1)}, bf16[64,2048]{1,0:T(8,128)(2,1)}, u32[]{:S(2)}) copy-start(bf16[64,2048]{1,0:T(8,128)(2,1)} %param.7) | copy-start | bytes 786436
  7.2 64.7 %copy-start.3 = (bf16[2048]{0:T(1024)(128)(2,1)S(1)}, bf16[2048]{0:T(1024)(128)(2,1)}, u32[]{:S(2)}) copy-start(bf16[2048]{0:T(1024)(128)(2,1)} %param.8) | copy-start | bytes 12292
  7.2 65.0 %copy-start.4 = (bf16[2048]{0:T(1024)(128)(2,1)S(1)}, bf16[2048]{0:T(1024)(128)(2,1)}, u32[]{:S(2)}) copy-start(bf16[2048]{0:T(1024)(128)(2,1)} %param.9) | copy-start | bytes 12292
  7.2 65.4 %copy-start.5 = (bf16[2048]{0:T(1024)(128)(2,1)S(1)}, bf16[2048]{0:T(1024)(128)(2,1)}, u32[]{:S(2)}) copy-start(bf16[2048]{0:T(1024)(128)(2,1)} %param.10) | copy-start | bytes 12292
  59.5 27.8 %all-to-all-start.1 = ((s32[1,32,128]{2,0,1:T(1,128)}), s32[1,32,128]{2,0,1:T(1,128)S(1)}, u32[]{:S(2)}, u32[]{:S(2)}) async-start(s32[1,32,128]{2,0,1:T(1,128)} %bitcast.12), calls=%async_computation.1 | async-start | bytes 32768 | tf_op jit(solution)/shard_map/all_to_all | solution.py:51
  87.3 25.8 %all-to-all-start = ((bf16[67,32,128]{2,0,1:T(8,128)(2,1)}), bf16[67,32,128]{2,0,1:T(8,128)(2,1)S(1)}, u32[]{:S(2)}, u32[]{:S(2)}) async-start(bf16[67,32,128]{2,0,1:T(8,128)(2,1)} %select_select_fusion), calls=%async_computation | async-start | bytes 1179648 | tf_op jit(solution)/shard_map/all_to_all | solution.py:50
  96.6 151.9 %all-gather.2.cloned.1.call-start = ((), (), s32[]{:S(2)}) async-start(), calls=%async_computation.3 | async-start | bytes 12976128 | tf_op jit(solution)/shard_map/all_gather | solution.py:61
Sparse Core Ops, SparseCore 0:
  127.3 121.1 all-gather.1
where the time goes:
time: 288 us; the launch traced here: 287 us
  waiting for transfers between devices  137 us (48%)
  local copies, waits for them, and re-layouts  54.7 us (19%)
  blocking collectives  23 us (8%)
  matrix products  22.1 us (8%)
  starting transfers between devices  21.3 us (7%)
  other arithmetic  15 us (5%)
  between operations  14.3 us (5%)
    all_gather x1, waiting for transfers between devices, on_device(): everyone = lax.all_gather(exposure, 'cpty', axis=1, tiled=True)  121 us
    gather x1, local copies, waits for them, and re-layouts, on_device(): labels = jnp.where(filled, trade_cpty[chosen], -1)[None, :]  23 us
    all_to_all x1, blocking collectives, summed_on_arrival(): lax.all_to_all(parts, axis, split_axis=0, concat_axis=0, tiled=True)  23 us
    all_to_all x1, waiting for transfers between devices, on_device(): lax.all_to_all(packed, 'cpty', split_axis=1, concat_axis=1, tiled=True)  15.6 us
    dot_general x1, matrix products, on_device(): netted = jnp.dot(arrived, onehot, preferred_element_type=jnp.float32)  14 us
    gather x2, local copies, waits for them, and re-layouts, on_device(): jnp.take(described, chosen, axis=1)  12.8 us
    all_to_all x1, starting transfers between devices, on_device(): lax.all_to_all(labels, 'cpty', split_axis=1, concat_axis=1, tiled=True)  12 us
    another operation x3, other arithmetic  9.41 us
  transfers between devices with their start and end apart: 3, of which 2 were waited for; matrix products, arithmetic and copies ran while one was open for 6% of the time, Pallas kernels for 0%

commit v1 on v0

--- a/solution.py
+++ b/solution.py
@@ -58,7 +58,10 @@
     )
     netted = jnp.dot(arrived, onehot, preferred_element_type=jnp.float32)
     exposure = jnp.maximum(netted, 0.0).astype(jnp.bfloat16)
-    everyone = lax.all_gather(exposure, "cpty", axis=1, tiled=True)
+    size = lax.axis_size("cpty")
+    pieces = jnp.stack([exposure for _ in range(size)])
+    pieces = lax.all_to_all(pieces, "cpty", split_axis=0, concat_axis=0)
+    everyone = jnp.concatenate(pieces, axis=1)
     path_total = exposure.shape[0] * lax.axis_size("paths")
     moment = (
         summed_on_arrival(

time: 288 us -> 432 us (1.50)
  blocking collectives: 23 us -> 302 us
  waiting for transfers between devices: 137 us -> 15.6 us
  between operations: 14.3 us -> 0.93 us
  local copies, waits for them, and re-layouts: 54.7 us -> 60.8 us
  matrix products: 22.1 us -> 16.8 us
    all_to_all x0 -> x1, blocking collectives: none -> 279 us  [on_device(): pieces = lax.all_to_all(pieces, 'cpty', split_axis=0, concat_axis=0)]
    all_gather x1 -> x0, waiting for transfers between devices: 121 us -> none  [on_device(): everyone = lax.all_gather(exposure, 'cpty', axis=1, tiled=True)]
    another operation x1 -> x2, local copies, waits for them, and re-layouts: 0.24 us -> 6.22 us  [the longest x1 5.99 us: on_device(): pieces = jnp.stack([exposure for _ in range(size)])]
    dot_general x1, matrix products: 8.06 us -> 3.61 us  [on_device(): jnp.einsum('pa,pb->ab', everyone, exposure, preferred_element_type=jnp.fl...]
  transfers between devices with their start and end apart: 3 -> 2, of which waited for: 2 -> 1; matrix products, arithmetic and copies ran while one was open for 6% -> 4% of each run, Pallas kernels for 0% -> 0%
where the time goes in v1:
time: 432 us
  blocking collectives  302 us (70%)
  local copies, waits for them, and re-layouts  60.8 us (14%)
  starting transfers between devices  21.2 us (5%)
  matrix products  16.8 us (4%)
  waiting for transfers between devices  15.6 us (4%)
  other arithmetic  15 us (3%)
    all_to_all x1, blocking collectives, on_device(): pieces = lax.all_to_all(pieces, 'cpty', split_axis=0, concat_axis=0)  279 us
    gather x1, local copies, waits for them, and re-layouts, on_device(): labels = jnp.where(filled, trade_cpty[chosen], -1)[None, :]  23 us
    all_to_all x1, blocking collectives, summed_on_arrival(): lax.all_to_all(parts, axis, split_axis=0, concat_axis=0, tiled=True)  22.4 us
    all_to_all x1, waiting for transfers between devices, on_device(): lax.all_to_all(packed, 'cpty', split_axis=1, concat_axis=1, tiled=True)  15.6 us
    dot_general x1, matrix products, on_device(): netted = jnp.dot(arrived, onehot, preferred_element_type=jnp.float32)  13.2 us
    gather x2, local copies, waits for them, and re-layouts, on_device(): jnp.take(described, chosen, axis=1)  12.7 us
    all_to_all x1, starting transfers between devices, on_device(): lax.all_to_all(labels, 'cpty', split_axis=1, concat_axis=1, tiled=True)  12 us
    another operation x3, other arithmetic  9.41 us
  transfers between devices with their start and end apart: 2, of which 1 were waited for; matrix products, arithmetic and copies ran while one was open for 4% of the time, Pallas kernels for 0%

profile of v1, /device:TPU:1, one launch (start us, length us, event | category | flops | bytes accessed | tf_op | source)
XLA Modules:
  0.0 432.0 jit_solution(14511910691201038168)
XLA Ops:
  0.7 0.8 add_select_fusion
  1.5 9.1 %reduce-window.6 = s32[32,16,128]{2,1,0:T(8,128)S(1)} reduce-window(s32[32,16,128]{2,1,0:T(8,128)S(1)} %fusion.18, s32[]{:T(128)} %constant.24.clone.1), window={size=1x1x128 pad=0_0x0_0x127_0}, to_apply=%region_0.1 | reduce-window | flops 8323072 | bytes 524292 | tf_op jit(solution)/shard_map/reduce-window
  10.6 0.1 slice.40
  10.7 0.2 copy.36
  11.0 0.2 reduce-window.9
  11.1 0.1 broadcast_add_fusion
  11.3 0.1 fusion.17
  11.4 0.7 compare_select_fusion.1
  12.1 8.1 %scatter_custom_fusion.1 = s32[4096]{0:T(1024)S(1)} fusion(s32[2048]{0:T(1024)S(1)} %compare_select_fusion.1, s32[2048]{0:T(1024)S(1)} %iota.15, s32[]{:T(128)} %constant.24.clone.1), kind=kCustom, calls=%fused_computation.49 | custom fusion | bytes 16388 | tf_op jit(solution)/shard_map/scatter | solution.py:39
  20.2 23.0 %gather_fusion.1 = s32[4096]{0:T(1024)S(1)} fusion(s32[2048]{0:T(1024)S(1)} %copy-done.1, s32[4096]{0:T(1024)S(1)} %fusion.19), kind=kCustom, calls=%fused_computation.1 | custom fusion | bytes 49152 | tf_op jit(solution)/shard_map/gather | solution.py:42
  43.3 9.1 %scatter_custom_fusion = pred[4096]{0:T(1024)(128)(4,1)S(1)} fusion(s32[2048]{0:T(1024)S(1)} %compare_select_fusion.1, pred[2048]{0:T(1024)(128)(4,1)S(1)} %broadcast.51, pred[]{:T(512)} %constant.22.clone.1), kind=kCustom, calls=%fused_computation.53 | custom fusion | bytes 4097 | tf_op jit(solution)/shard_map/scatter | solution.py:41
  52.4 0.6 broadcast_select_fusion
  53.0 12.0 %all-to-all-start.1 = ((s32[1,32,128]{2,0,1:T(1,128)}), s32[1,32,128]{2,0,1:T(1,128)S(1)}, u32[]{:S(2)}, u32[]{:S(2)}) async-start(s32[1,32,128]{2,0,1:T(1,128)} %bitcast.12), calls=%async_computation.1 | async-start | bytes 32768 | tf_op jit(solution)/shard_map/all_to_all | solution.py:51
  65.1 0.3 copy.28
  65.4 0.3 stack.12
  65.7 0.3 stack.13
  66.1 0.3 stack.14
  66.4 0.7 pad_maximum_fusion
  67.1 12.1 %gather_fusion = bf16[4096,67]{1,0:T(8,128)(2,1)S(1)} fusion(bf16[67,2048]{0,1:T(8,128)(2,1)S(1)} %pad_maximum_fusion, s32[4096]{0:T(1024)S(1)} %fusion.19), kind=kCustom, calls=%fused_computation | custom fusion | bytes 1114112 | tf_op jit(solution)/shard_map/jit(_take)/gather | solution.py:47
  79.2 0.6 copy.32
  79.8 0.9 select_select_fusion
  80.8 9.2 %all-to-all-start = ((bf16[67,32,128]{2,0,1:T(8,128)(2,1)}), bf16[67,32,128]{2,0,1:T(8,128)(2,1)S(1)}, u32[]{:S(2)}, u32[]{:S(2)}) async-start(bf16[67,32,128]{2,0,1:T(8,128)(2,1)} %select_select_fusion), calls=%async_computation | async-start | bytes 1179648 | tf_op jit(solution)/shard_map/all_to_all | solution.py:50
  90.0 0.9 iota_compare_fusion.7
  90.9 15.6 %all-to-all-done = bf16[67,32,128]{2,0,1:T(8,128)(2,1)S(1)} async-done(((bf16[67,32,128]{2,0,1:T(8,128)(2,1)}), bf16[67,32,128]{2,0,1:T(8,128)(2,1)S(1)}, u32[]{:S(2)}, u32[]{:S(2)}) %all-to-all-start) | async-done | bytes 548896 | tf_op jit(solution)/shard_map/all_to_all | solution.py:50
  106.6 13.2 %fusion.9 = bf16[1536,128]{1,0:T(8,128)(2,1)S(1)} fusion(bf16[64,1536]{1,0:T(8,128)(2,1)S(1)} %copy-done, f32[4096]{0:T(1024)S(1)} %get-tuple-element.3, f32[4096]{0:T(1024)S(1)} %get-tuple-element.4, f32[4096]{0:T(1024)S(1)} %get-tuple-element.2, bf16[67,32,128]{2,0,1:T(8,128)(2,1)S(1)} %all-to-all-done, pred[4096,128]{1,0:T(32,128)(4,1)S(1)} %iota_compare_fusion.7), kind=kOutput, calls=%fused_computation.16 | convolution fusion | flops 2447769600 | bytes 1687552 | tf_op jit(solution)/shard_map/dot_general | solution.py:59
  119.8 0.2 copy.35
  120.0 6.0 %stack.11 = bf16[32,1536,128]{1,2,0:T(8,128)(2,1)} broadcast(bf16[1536,128]{0,1:T(8,128)(2,1)S(1)} %copy.35), dimensions={1,2} | broadcast | bytes 12976128 | tf_op jit(solution)/shard_map/stack | solution.py:62
  126.0 279.1 %all_to_all.25 = bf16[32,1536,128]{1,2,0:T(8,128)(2,1)S(1)} all-to-all(bf16[32,1536,128]{1,2,0:T(8,128)(2,1)} %stack.11), channel_id=1, replica_groups=mesh['paths'=8,'cpty'=32] {'cpty'}, dimensions={0} | all-to-all | bytes 25165824 | tf_op jit(solution)/shard_map/all_to_all | solution.py:63
  405.1 3.6 convolution_convert_fusion
  408.8 22.4 %all_to_all.26 = bf16[8,512,128]{2,1,0:T(8,128)(2,1)S(1)} all-to-all(bf16[8,512,128]{2,1,0:T(8,128)(2,1)S(1)} %bitcast.90), channel_id=1, replica_groups=mesh['paths'=8,'cpty'=32] {'paths'}, dimensions={0} | all-to-all | bytes 2097152 | tf_op jit(solution)/shard_map/all_to_all | solution.py:16
  431.1 0.1 convert_reduce_fusion
  431.3 0.7 broadcast_multiply_fusion
  (24 shorter events, 0.1 us)
Async XLA Ops:
  0.6 105.9 %copy-start = (bf16[64,1536]{1,0:T(8,128)(2,1)S(1)}, bf16[64,1536]{1,0:T(8,128)(2,1)}, u32[]{:S(2)}) copy-start(bf16[64,1536]{1,0:T(8,128)(2,1)} %param.6) | copy-start | bytes 589828
  0.6 19.6 %copy-start.1 = (s32[2048]{0:T(1024)S(1)}, s32[2048]{0:T(1024)}, u32[]{:S(2)}) copy-start(s32[2048]{0:T(1024)} %param.11) | copy-start | bytes 24580
  0.7 64.4 %copy-start.3 = (bf16[64,2048]{1,0:T(8,128)(2,1)S(1)}, bf16[64,2048]{1,0:T(8,128)(2,1)}, u32[]{:S(2)}) copy-start(bf16[64,2048]{1,0:T(8,128)(2,1)} %param.7) | copy-start | bytes 786436
  0.7 64.7 %copy-start.4 = (bf16[2048]{0:T(1024)(128)(2,1)S(1)}, bf16[2048]{0:T(1024)(128)(2,1)}, u32[]{:S(2)}) copy-start(bf16[2048]{0:T(1024)(128)(2,1)} %param.8) | copy-start | bytes 12292
  0.7 65.0 %copy-start.5 = (bf16[2048]{0:T(1024)(128)(2,1)S(1)}, bf16[2048]{0:T(1024)(128)(2,1)}, u32[]{:S(2)}) copy-start(bf16[2048]{0:T(1024)(128)(2,1)} %param.9) | copy-start | bytes 12292
  0.7 65.4 %copy-start.6 = (bf16[2048]{0:T(1024)(128)(2,1)S(1)}, bf16[2048]{0:T(1024)(128)(2,1)}, u32[]{:S(2)}) copy-start(bf16[2048]{0:T(1024)(128)(2,1)} %param.10) | copy-start | bytes 12292
  53.0 27.7 %all-to-all-start.1 = ((s32[1,32,128]{2,0,1:T(1,128)}), s32[1,32,128]{2,0,1:T(1,128)S(1)}, u32[]{:S(2)}, u32[]{:S(2)}) async-start(s32[1,32,128]{2,0,1:T(1,128)} %bitcast.12), calls=%async_computation.1 | async-start | bytes 32768 | tf_op jit(solution)/shard_map/all_to_all | solution.py:51
  80.8 25.8 %all-to-all-start = ((bf16[67,32,128]{2,0,1:T(8,128)(2,1)}), bf16[67,32,128]{2,0,1:T(8,128)(2,1)S(1)}, u32[]{:S(2)}, u32[]{:S(2)}) async-start(bf16[67,32,128]{2,0,1:T(8,128)(2,1)} %select_select_fusion), calls=%async_computation | async-start | bytes 1179648 | tf_op jit(solution)/shard_map/all_to_all | solution.py:50
  119.8 285.3 %copy-start.2 = (bf16[1536,128]{1,0:T(8,128)(2,1)}, bf16[1536,128]{1,0:T(8,128)(2,1)S(1)}, u32[]{:S(2)}) copy-start(bf16[1536,128]{1,0:T(8,128)(2,1)S(1)} %fusion.9) | copy-start | bytes 1179652
